TPU v7x, 32 devices: a whole 2x2x4 slice. The times are simulated.
32 devices in a mesh: lat: 4 (over z), lon: 4 (over y, x), obs: 2 (over core).
Axes of the slice: x: 2, y: 2, z: 4, core: 2. Of those that a mesh axis runs over, the one named last changes fastest.
Arguments:
- innovation: float32 [4096, 128], P(('lat', 'lon', 'obs')), may hold values from -6 to 6
- obs_error: float32 [4096, 128], P(('lat', 'lon', 'obs')), may hold values from 0.5 to 2
- obs_offset: float32 [2, 4096, 128], P(None, ('lat', 'lon', 'obs')), may hold values from 0 to 1
- obs_cell: int32 [4096, 128], P(('lat', 'lon', 'obs')), may hold values from 0 to 65535
- obs_owner: int32 [32, 128], P(('lat', 'lon', 'obs')), may hold values from 0 to 15, as said below
- block_count: int32 [32], P(('lat', 'lon', 'obs')), may hold values from 64 to 128
- land_mask: int32 [256, 4096], P(('lat', 'obs'), 'lon'), may hold values from 0 to 1, as said below
- inertia: float32 [256, 4096], P(('lat', 'obs'), 'lon'), may hold values from 0.002 to 0.05
- sea_depth: float32 [256, 4096], P(('lat', 'obs'), 'lon'), may hold values from 0.5 to 5
Outputs:
- adjoint_field: float32 [256, 4096], P(('lat', 'obs'), 'lon')
- residual: float32 [256, 4096], P(('lat', 'obs'), 'lon')
Inputs may be any that keep to these rules, and one draw needn't show every extreme that they name: `obs_owner`: among the live blocks of one device at most 16 name the same tile; in every draw some tile is named by exactly 16 live blocks of every device. `land_mask`: the first and the last grid row are land.
All inputs are finite; a program needn't handle non-finite values.
Results may differ from a plain program's by a relative error of at most 0.0003.
Values sent between devices are 32-bit elements; how exact they have to be, the bound alone decides.
A program may use at most 64 MiB of HBM per device.

v0:
```python
import functools

import jax
import jax.numpy as jnp
from jax import lax
from jax.experimental import pallas as pl
from jax.experimental.pallas import tpu as pltpu
from jax.sharding import PartitionSpec as P

ITERS = 5
ROW_PAD = 8
COL_PAD = 128
FINE_ROW = 16
FINE_COL = 8
MESH = pl.DeviceIdType.MESH
AXES = ("lat", "lon", "obs")
F32 = jnp.float32
BF16 = jnp.bfloat16


def iota(shape, axis):
    return lax.broadcasted_iota(jnp.int32, shape, axis)


def moved(value, axis, back):
    size = value.shape[axis]
    return pltpu.roll(value, size - 1 if back else 1, axis)


def fine_size():
    return -(-(FINE_ROW + 1) * (FINE_COL + 1) // 16) * 16


def spread_block(capacity, width, cols, coarse, block):
    fine = fine_size()
    amount = block[:, :width]
    north = block[:, width : 2 * width]
    east = block[:, 2 * width : 3 * width]
    cell = block[:, 3 * width :]
    row = jnp.floor(cell * (1.0 / cols))
    col = cell - row * cols
    row_group = jnp.floor(row * (1.0 / FINE_ROW))
    col_group = jnp.floor(col * (1.0 / FINE_COL))
    step = FINE_ROW + 1
    first = (col - col_group * FINE_COL) * step + (row - row_group * FINE_ROW)
    group = row_group * (cols // FINE_COL) + col_group - coarse // 2
    upper = amount * (1.0 - north)
    lower = amount * north
    corners = []
    for shift, part in (
        (0, upper * (1.0 - east)),
        (1, lower * (1.0 - east)),
        (step, upper * east),
        (step + 1, lower * east),
    ):
        high = part.astype(BF16).astype(F32)
        corners.append((first + shift, high, part - high))

    def wide(values, slot, count):
        tile = jnp.broadcast_to(values[slot : slot + 1], (16, width)).astype(BF16)
        return jnp.concatenate([tile] * (count // 16), axis=0)

    fine_axis = iota((fine, width), 0).astype(F32).astype(BF16)
    coarse_axis = (iota((coarse, width), 0) - coarse // 2).astype(F32).astype(BF16)
    zero = jnp.zeros((), BF16)
    one = jnp.ones((), BF16)
    left, right = [], []
    for slot in range(capacity):
        high = low = zero
        for place, top, rest in corners:
            hit = fine_axis == wide(place, slot, fine)
            high = jnp.where(hit, wide(top, slot, fine), high)
            low = jnp.where(hit, wide(rest, slot, fine), low)
        left.append(jnp.concatenate([high, low], axis=0))
        right.append(jnp.where(coarse_axis == wide(group, slot, coarse), one, zero))
    return lax.dot_general(
        jnp.concatenate(left, axis=1),
        jnp.concatenate(right, axis=1),
        (((1,), (1,)), ((), ())),
        preferred_element_type=F32,
    )


def kernel(
    capacity,
    innov_hbm, error_hbm, offset_hbm, cell_hbm, owner_hbm, count_ref, land_hbm, inertia_hbm, depth_hbm,
    x_ref, r_ref,
    innov_ref, error_ref, offset_ref, cell_ref, owner_ref, land_ref, depth_ref, ground_ref,
    sent_ref, inbox_ref, acc_ref, perm_ref,
    tile_ref, pack_ref, strip_ref, pair_ref, edge_ref, side_ref,
    up_ref, down_ref, mid_ref, cwest_ref, ceast_ref,
    ocean_ref, diag_ref, cn_ref, cs_ref, cw_ref, ce_ref, q_ref,
    part_ref, slot_ref, gram_ref,
    in_sem, send_sem, recv_sem, halo_send, halo_recv, swap_send, swap_recv, sum_send, sum_recv,
):
    n_lat, n_lon, n_obs = (lax.axis_size(name) for name in AXES)
    lat, lon, core = (lax.axis_index(name) for name in AXES)
    tiles = n_lat * n_lon
    total = tiles * n_obs
    me = (lat * n_lon + lon) * n_obs + core
    rows, cols = x_ref.shape
    tall = rows + 2 * ROW_PAD
    keep = rows + ROW_PAD
    tile_rows = rows * n_obs
    blocks, width = innov_ref.shape
    cap_pad = sent_ref.shape[1]
    fine = fine_size()
    coarse = acc_ref.shape[1]
    group_cols = cols // FINE_COL

    def place(flat):
        return (flat // (n_lon * n_obs), (flat // n_obs) % n_lon, flat % n_obs)

    loads = [
        pltpu.make_async_copy(source, target, in_sem.at[number])
        for number, (source, target) in enumerate(
            (
                (owner_hbm, owner_ref),
                (innov_hbm, innov_ref),
                (error_hbm, error_ref),
                (offset_hbm, offset_ref),
                (cell_hbm, cell_ref),
                (land_hbm, land_ref),
                (depth_hbm, depth_ref),
                (inertia_hbm, ground_ref.at[1]),
            )
        )
    ]
    for load in loads:
        load.start()

    barrier = pltpu.get_barrier_semaphore()

    def greet(k, carry):
        pl.semaphore_signal(
            barrier, inc=1, device_id=place(lax.rem(me + k, total)), device_id_type=MESH
        )
        return carry

    lax.fori_loop(1, total, greet, 0)

    loads[0].wait()
    count = count_ref[0]
    owner_row = jnp.broadcast_to(owner_ref[...].astype(F32), (blocks, blocks))
    owner_col = owner_row.T
    earlier = (iota((blocks, blocks), 0) < iota((blocks, blocks), 1)) & (
        iota((blocks, blocks), 0) < count
    )
    same = jnp.where((owner_row == owner_col) & earlier, 1.0, 0.0)
    rank = jnp.sum(same, axis=0, keepdims=True)
    slot_of = owner_row[:1] * cap_pad + rank
    slot_of = jnp.where(iota((1, blocks), 1) < count, slot_of, -1.0)
    slots = tiles * cap_pad
    chosen = iota((slots, blocks), 0).astype(F32) == slot_of
    chosen = jnp.where(chosen, 1.0, 0.0).astype(BF16)
    for load in loads[1:5]:
        load.wait()
    error = error_ref[...]
    data = jnp.concatenate(
        [
            innov_ref[...] / (error * error),
            offset_ref[0],
            offset_ref[1],
            cell_ref[...].astype(F32),
        ],
        axis=1,
    )
    high = data.astype(BF16)
    rest = data - high.astype(F32)
    middle = rest.astype(BF16)
    low = (rest - middle.astype(F32)).astype(BF16)
    sent_ref[...] = jnp.dot(
        jnp.concatenate([chosen] * 3, axis=1),
        jnp.concatenate([high, middle, low], axis=0),
        preferred_element_type=F32,
    ).reshape(sent_ref.shape)
    for load in loads[5:]:
        load.wait()
    ground_ref[0] = land_ref[...].astype(F32) * depth_ref[...]
    pl.semaphore_wait(barrier, total - 1)

    def turn_of(k):
        ring_step, shift = k // n_lon, k % n_lon
        odd = ring_step % 2
        hop = odd * ((ring_step + 1) // 2) + (1 - odd) * (n_lat - ring_step // 2)
        return hop % n_lat, shift

    def block_copy(k):
        hop, shift = turn_of(k)
        to_lat, to_lon = (lat + hop) % n_lat, (lon + shift) % n_lon
        return pltpu.make_async_remote_copy(
            src_ref=sent_ref.at[to_lat * n_lon + to_lon],
            dst_ref=inbox_ref.at[k],
            send_sem=send_sem.at[k],
            recv_sem=recv_sem.at[k],
            device_id=(to_lat, to_lon, core),
            device_id_type=MESH,
        )

    def send(k, carry):
        block_copy(tiles - k).start()
        return carry

    lax.fori_loop(1, tiles, send, 0)

    def halo_copy(index, source, target, device):
        return pltpu.make_async_remote_copy(
            src_ref=source,
            dst_ref=target,
            send_sem=halo_send.at[index],
            recv_sem=halo_recv.at[index],
            device_id=device,
            device_id_type=MESH,
        )

    ring = n_lat * n_obs
    line = lat * n_obs + core
    above = lax.rem(line + ring - 1, ring)
    below = lax.rem(line + 1, ring)
    west = lax.rem(lon + n_lon - 1, n_lon)
    east = lax.rem(lon + 1, n_lon)
    to_below = halo_copy(
        0, ground_ref.at[:, pl.ds(rows - ROW_PAD, ROW_PAD)], up_ref, (below // n_obs, lon, below % n_obs)
    )
    to_above = halo_copy(
        1, ground_ref.at[:, pl.ds(0, ROW_PAD)], down_ref, (above // n_obs, lon, above % n_obs)
    )
    to_east = halo_copy(2, mid_ref.at[:, :, pl.ds(cols - COL_PAD, COL_PAD)], cwest_ref, (lat, east, core))
    to_west = halo_copy(3, mid_ref.at[:, :, pl.ds(0, COL_PAD)], ceast_ref, (lat, west, core))
    to_below.start()
    to_above.start()

    def post_sum(turn, parts):
        stack = jnp.concatenate(
            parts + [jnp.zeros((COL_PAD - 8 * len(parts), COL_PAD), F32)], axis=0
        )
        values = jnp.sum(stack.T, axis=0, keepdims=True)
        slot_ref[turn, pl.ds(me, 1)] = values[None]
        part_ref[turn] = values

        def post(k, carry):
            pltpu.make_async_remote_copy(
                src_ref=part_ref.at[turn],
                dst_ref=slot_ref.at[turn, me],
                send_sem=sum_send.at[turn],
                recv_sem=sum_recv.at[turn],
                device_id=place(lax.rem(me + k, total)),
                device_id_type=MESH,
            ).start()
            return carry

        lax.fori_loop(1, total, post, 0)

    def take_sum(turn, number):
        block = slot_ref.at[turn, pl.ds(0, total - 1)]
        pltpu.make_async_copy(block, block, sum_recv.at[turn]).wait()
        pltpu.make_async_copy(block, block, sum_send.at[turn]).wait()
        values = jnp.sum(slot_ref[turn], axis=0)
        gram_ref[...] = jnp.broadcast_to(values, (COL_PAD, COL_PAD)).T
        return [
            jnp.sum(gram_ref[8 * k : 8 * k + 8], axis=0, keepdims=True) for k in range(number)
        ]

    def inner(value):
        return value[ROW_PAD:keep, :cols]

    def fold(value):
        out = value[:8]
        for start in range(8, rows, 8):
            out = out + value[start : start + 8]
        lanes = out[:, :COL_PAD]
        for start in range(COL_PAD, cols, COL_PAD):
            lanes = lanes + out[:, start : start + COL_PAD]
        return lanes

    def spread(k):
        return spread_block(capacity, width, cols, coarse, k)

    acc_ref[...] = spread(sent_ref[lat * n_lon + lon])

    def fill(part, carry):
        shape = (group_cols, cols)
        target = iota(shape, 0) * FINE_COL + part
        start = pl.multiple_of(part * group_cols, group_cols)
        perm_ref[pl.ds(start, group_cols)] = jnp.where(target == iota(shape, 1), 1.0, 0.0).astype(BF16)
        return carry

    lax.fori_loop(0, FINE_COL, fill, 0)

    def turn(k, carry):
        block_copy(k).wait_recv()
        acc_ref[...] = acc_ref[...] + spread(inbox_ref[k])

        @pl.when(k == tiles // 4 - 1)
        def _():
            to_below.wait()
            to_above.wait()
            mid_ref[:, :ROW_PAD] = up_ref[...]
            mid_ref[:, ROW_PAD:keep] = ground_ref[...]
            mid_ref[:, keep:] = down_ref[...]
            to_east.start()
            to_west.start()

        @pl.when(k == tiles // 2 - 1)
        def _():
            to_east.wait()
            to_west.wait()
            near = iota((tall, COL_PAD), 1) < COL_PAD // 2

            def widened(index):
                pad = jnp.where(near, ceast_ref[index], cwest_ref[index])
                return jnp.concatenate([mid_ref[index], pad], axis=1)

            conduct = widened(0)
            cn = jnp.sqrt(conduct * moved(conduct, 0, False))
            cs = moved(cn, 0, True)
            cw = jnp.sqrt(conduct * moved(conduct, 1, False))
            ce = moved(cw, 1, True)
            ocean = jnp.where(conduct > 0.0, 1.0, 0.0)
            diag = widened(1) + cn + cs + cw + ce
            cn_ref[...] = cn
            cs_ref[...] = cs
            cw_ref[...] = cw
            ce_ref[...] = ce
            ocean_ref[...] = ocean
            diag_ref[...] = diag
            kept = inner(diag) * inner(ocean)
            faces = cn * cn + cs * cs + cw * cw + ce * ce
            post_sum(0, [fold(inner(ocean)), fold(kept), fold(kept * kept), fold(inner(faces))])

        return carry

    lax.fori_loop(1, tiles, turn, 0)

    acc_ref[:fine] = acc_ref[:fine] + acc_ref[fine:]
    step = FINE_ROW + 1
    top_row = iota((8, group_cols), 0) == 0
    blank = jnp.zeros((FINE_ROW - 8, group_cols), F32)
    planes = []
    for part in range(FINE_COL + 1):
        pieces, spill = [], None
        for index in range(tile_rows // FINE_ROW):
            lanes = slice(index * group_cols, (index + 1) * group_cols)
            piece = acc_ref[part * step : part * step + FINE_ROW, lanes]
            if spill is not None:
                piece = piece + jnp.concatenate([spill, blank], axis=0)
            pieces.append(piece)
            last = acc_ref[part * step + FINE_ROW : part * step + step, lanes]
            spill = jnp.where(top_row, last, 0.0)
        planes.append(jnp.concatenate(pieces + [spill], axis=0))
    over = pltpu.roll(planes[FINE_COL], 1, 1)
    lane = iota(over.shape, 1)
    planes[0] = planes[0] + jnp.where(lane > 0, over, 0.0)
    beyond = jnp.where(lane == 0, over, 0.0)
    mixed = jnp.concatenate(planes[:FINE_COL], axis=1)
    high = mixed.astype(BF16).astype(F32)
    mixed = jnp.concatenate([high, mixed - high], axis=0).astype(BF16)
    natural = jnp.dot(mixed, perm_ref[...], preferred_element_type=F32)
    tile_tall = tile_rows + ROW_PAD
    natural = natural[:tile_tall] + natural[tile_tall:]
    tile_ref[:, :cols] = natural
    tile_ref[:, cols:] = beyond
    top = iota((ROW_PAD, cols + COL_PAD), 0) == 0
    pack_ref[...] = jnp.where(
        top, tile_ref[tile_rows:], tile_ref[tile_rows - ROW_PAD : tile_rows]
    )
    sides = jnp.where(lane < COL_PAD // 2, natural[:, :COL_PAD], natural[:, cols - COL_PAD :])
    sides = jnp.where(lane == COL_PAD - 8, pltpu.roll(beyond, COL_PAD - 8, 1), sides)
    sides = jnp.concatenate([sides, jnp.zeros((COL_PAD - tile_tall, COL_PAD), F32)], axis=0)
    strip_ref[...] = sides.T

    split = rows - ROW_PAD
    mine = pl.multiple_of(core * split, 8)
    theirs = pl.multiple_of((1 - core) * split, 8)
    north = lat > 0
    south = lat < n_lat - 1
    from_west = strip_ref.at[pl.ds(0, 8)]
    from_east = strip_ref.at[pl.ds(COL_PAD - 8, 8)]

    def swap_copy(out, into, source, target, device):
        return pltpu.make_async_remote_copy(
            src_ref=source,
            dst_ref=target,
            send_sem=swap_send.at[out],
            recv_sem=swap_recv.at[into],
            device_id=device,
            device_id_type=MESH,
        )

    up_lat, down_lat = jnp.maximum(lat - 1, 0), jnp.minimum(lat + 1, n_lat - 1)

    def northern():
        return [
            swap_copy(1, 1 + core, tile_ref.at[pl.ds(0, 8)], edge_ref.at[core], (up_lat, lon, 1)),
            swap_copy(2, 3 + core, from_west, side_ref.at[2 + core], (up_lat, west, 1)),
            swap_copy(3, 5 + core, from_east, side_ref.at[6 + core], (up_lat, east, 1)),
        ]

    def southern():
        return [
            swap_copy(4, 1 + core, pack_ref, edge_ref.at[core], (down_lat, lon, 0)),
            swap_copy(5, 3 + core, from_west, side_ref.at[2 + core], (down_lat, west, 0)),
            swap_copy(6, 5 + core, from_east, side_ref.at[6 + core], (down_lat, east, 0)),
        ]

    level = [
        swap_copy(7 + peer, 7 + core, from_west, side_ref.at[core], (lat, west, peer))
        for peer in range(2)
    ] + [
        swap_copy(9 + peer, 9 + core, from_east, side_ref.at[4 + core], (lat, east, peer))
        for peer in range(2)
    ]
    swap = swap_copy(0, 0, tile_ref.at[pl.ds(theirs, tall)], pair_ref, (lat, lon, 1 - core))

    @pl.when(north)
    def _():
        for item in northern():
            item.start()

    @pl.when(south)
    def _():
        for item in southern():
            item.start()

    for item in level:
        item.start()
    swap.start()

    ocean_count, diag_sum, diag_square, face_square = take_sum(0, 4)
    ocean_count = jnp.maximum(ocean_count, 1.0)
    mean = diag_sum / ocean_count
    spread_out = jnp.maximum((diag_square + face_square) / ocean_count - mean * mean, 0.0)
    mean = 1.2 * mean

    def across(value, size):
        return jnp.concatenate([value] * (size // COL_PAD), axis=1)

    diag_ref[...] = diag_ref[...] - across(mean, cols + COL_PAD)

    linked = jnp.where(core == 0, lat, n_lat - 1 - lat) > 0

    def arrived(number, target):
        return swap_copy(0, number, target, target, (lat, lon, 1 - core))

    @pl.when(linked)
    def _():
        for sender in range(2):
            arrived(1 + sender, edge_ref.at[sender]).wait_recv()
            arrived(3 + sender, side_ref.at[2 + sender]).wait_recv()
            arrived(5 + sender, side_ref.at[6 + sender]).wait_recv()

    @pl.when(jnp.logical_not(linked))
    def _():
        edge_ref[...] = jnp.zeros_like(edge_ref)
        side_ref[2:4] = jnp.zeros((2, 8, COL_PAD), F32)
        side_ref[6:8] = jnp.zeros((2, 8, COL_PAD), F32)

    for sender in range(2):
        arrived(7 + sender, side_ref.at[sender]).wait_recv()
        arrived(9 + sender, side_ref.at[4 + sender]).wait_recv()

    def aligned(straight, corner):
        first = core == 0
        straight = jnp.where(
            first, pltpu.roll(straight, ROW_PAD, 1), pltpu.roll(straight, COL_PAD - split, 1)
        )
        corner = jnp.where(
            first,
            pltpu.roll(corner, COL_PAD - (tile_rows - ROW_PAD), 1),
            pltpu.roll(corner, keep, 1),
        )
        return straight + corner

    right_side = aligned(side_ref[0] + side_ref[1], side_ref[2] + side_ref[3])
    left_side = aligned(side_ref[4] + side_ref[5], side_ref[6] + side_ref[7])
    hole = jnp.zeros((COL_PAD - 16, COL_PAD), F32)
    beside = jnp.concatenate([right_side, hole, left_side], axis=0).T[:tall]
    entering = jnp.where(iota(beside.shape, 1) == 0, pltpu.roll(beside, 8, 1), 0.0)
    edge = edge_ref[0] + edge_ref[1]
    swap.wait_recv()

    @pl.when(core == 0)
    def _():
        q_ref[0, :ROW_PAD] = jnp.where(top, 0.0, edge)
        q_ref[0, ROW_PAD : 2 * ROW_PAD] = (
            tile_ref[:ROW_PAD] + pair_ref[:ROW_PAD] + jnp.where(top, edge, 0.0)
        )
        q_ref[0, 2 * ROW_PAD :] = tile_ref[ROW_PAD:keep] + pair_ref[ROW_PAD:keep]

    @pl.when(core == 1)
    def _():
        q_ref[0, :keep] = tile_ref[pl.ds(split, keep)] + pair_ref[:keep]
        q_ref[0, keep:] = tile_ref[pl.ds(split + keep, ROW_PAD)] + pair_ref[keep:] + edge

    q_ref[0, :, :COL_PAD] = q_ref[0, :, :COL_PAD] + entering
    q_ref[0, :, cols:] = q_ref[0, :, cols:] + beside
    q_ref[0] = q_ref[0] * ocean_ref[...]

    spread_wide = across(spread_out, cols + COL_PAD)
    for k in range(ITERS):
        field = q_ref[k]
        value = (
            diag_ref[...] * field
            - cn_ref[...] * moved(field, 0, False)
            - cs_ref[...] * moved(field, 0, True)
            - cw_ref[...] * moved(field, 1, False)
            - ce_ref[...] * moved(field, 1, True)
        )
        if k:
            value = value - spread_wide * q_ref[k - 1]
        q_ref[k + 1] = value

    fields = [q_ref[k, ROW_PAD:keep, :cols] for k in range(ITERS + 1)]
    pairs = [(k, k + d) for k in range(ITERS) for d in range(2)]
    post_sum(1, [fold(fields[i] * fields[j]) for i, j in pairs])
    sums = take_sum(1, len(pairs))
    gram = {}
    for (i, j), value in zip(pairs, sums):
        gram[i, j] = gram[j, i] = value
    for gap in range(1, ITERS):
        for i in range(ITERS - gap):
            j = i + gap
            value = gram[i + 1, j]
            if i:
                value = value + spread_out * (gram[i - 1, j] - gram[i, j - 1])
            else:
                value = value - spread_out * gram[i, j - 1]
            gram[i, j + 1] = gram[j + 1, i] = value

    def plus(one, two):
        if one is None or two is None:
            return two if one is None else one
        return one + two

    def times(weight, part):
        return None if part is None else weight * part

    def quad(first, second):
        out = None
        for i, one in enumerate(first):
            line = None
            for j, two in enumerate(second):
                if one is not None and two is not None:
                    line = plus(line, two * gram[i, j])
            out = plus(out, times(one, line) if one is not None else None)
        return out

    def apply(weights):
        out = [None] * (ITERS + 1)
        for k, weight in enumerate(weights[:ITERS]):
            if weight is not None:
                out[k + 1] = plus(out[k + 1], weight)
                out[k] = plus(out[k], mean * weight)
                if k:
                    out[k - 1] = plus(out[k - 1], spread_out * weight)
        return out

    unit = jnp.ones((1, COL_PAD), F32)
    direct = [unit] + [None] * ITERS
    resid = [unit] + [None] * ITERS
    gained = [None] * (ITERS + 1)
    norm = gram[0, 0]
    for done in range(1, ITERS + 1):
        applied = apply(direct)
        step_size = norm / quad(direct, applied)
        gained = [plus(one, times(step_size, two)) for one, two in zip(gained, direct)]
        resid = [plus(one, times(-step_size, two)) for one, two in zip(resid, applied)]
        if done < ITERS:
            norm_next = quad(resid, resid)
            ratio = norm_next / norm
            direct = [plus(one, times(ratio, two)) for one, two in zip(resid, direct)]
            norm = norm_next

    def mix(weights):
        out = None
        for k, weight in enumerate(weights):
            if weight is not None:
                out = plus(out, across(weight, cols) * q_ref[k, ROW_PAD:keep, :cols])
        return out

    x_ref[...] = mix(gained)
    r_ref[...] = mix(resid)

    def finish(k, carry):
        block_copy(k).wait_send()
        return carry

    lax.fori_loop(1, tiles, finish, 0)
    swap.wait_send()
    for item in level:
        item.wait_send()

    @pl.when(north)
    def _():
        for item in northern():
            item.wait_send()

    @pl.when(south)
    def _():
        for item in southern():
            item.wait_send()


def body(
    innovation, obs_error, obs_offset, obs_cell, obs_owner, block_count,
    land_mask, inertia, sea_depth,
):
    block_total = obs_owner.shape[1]
    width = innovation.shape[1]
    n_lat, n_lon, n_obs = (lax.axis_size(name) for name in AXES)
    tiles = n_lat * n_lon
    capacity = max(3, 2 * ((block_total + tiles - 1) // tiles))
    cap_pad = -(-capacity // 8) * 8
    rows, cols = land_mask.shape
    total = tiles * n_obs
    coarse = (rows * n_obs // FINE_ROW) * (cols // FINE_COL)
    tall, broad = rows + 2 * ROW_PAD, cols + COL_PAD
    tile_tall = rows * n_obs + ROW_PAD
    vmem = lambda *shape: pltpu.VMEM(shape, F32)
    whole = pl.BlockSpec(memory_space=pltpu.VMEM)
    far = pl.BlockSpec(memory_space=pltpu.HBM)
    near = pl.BlockSpec(memory_space=pltpu.SMEM)
    dma = pltpu.SemaphoreType.DMA
    return pl.pallas_call(
        functools.partial(kernel, capacity),
        out_shape=[jax.ShapeDtypeStruct((rows, cols), F32)] * 2,
        in_specs=[far] * 5 + [near] + [far] * 3,
        out_specs=[whole] * 2,
        scratch_shapes=[
            vmem(*innovation.shape),
            vmem(*obs_error.shape),
            vmem(*obs_offset.shape),
            pltpu.VMEM(obs_cell.shape, jnp.int32),
            pltpu.VMEM(obs_owner.shape, jnp.int32),
            pltpu.VMEM((rows, cols), jnp.int32),
            vmem(rows, cols),
            vmem(2, rows, cols),
            vmem(tiles, cap_pad, 4 * width),
            vmem(tiles, cap_pad, 4 * width),
            vmem(2 * fine_size(), coarse),
            pltpu.VMEM((cols, cols), BF16),
            vmem(tile_tall, broad),
            vmem(ROW_PAD, broad),
            vmem(COL_PAD, COL_PAD),
            vmem(tall, broad),
            vmem(2, ROW_PAD, broad),
            vmem(8, 8, COL_PAD),
            vmem(2, ROW_PAD, cols),
            vmem(2, ROW_PAD, cols),
            vmem(2, tall, cols),
            vmem(2, tall, COL_PAD),
            vmem(2, tall, COL_PAD),
        ]
        + [vmem(tall, broad)] * 6
        + [
            vmem(ITERS + 1, tall, broad),
            vmem(2, 1, COL_PAD),
            vmem(2, total, 1, COL_PAD),
            vmem(COL_PAD, COL_PAD),
            dma((8,)),
            dma((tiles,)),
            dma((tiles,)),
            dma((4,)),
            dma((4,)),
            dma((11,)),
            dma((11,)),
            dma((2,)),
            dma((2,)),
        ],
        compiler_params=pltpu.CompilerParams(collective_id=0, has_side_effects=True),
        name="adjoint",
    )(
        innovation, obs_error, obs_offset, obs_cell, obs_owner, block_count,
        land_mask, inertia, sea_depth,
    )


def solution(mesh):
    spread = P(AXES, None)
    grid = P(("lat", "obs"), "lon")
    in_specs = (spread, spread, P(None, AXES, None), spread, spread, P(AXES), grid, grid, grid)
    return jax.shard_map(
        body, mesh=mesh, in_specs=in_specs, out_specs=(grid, grid), check_vma=False
    )
```

profile of v0, /device:TPU:0, one launch (start us, length us, event | category | flops | bytes accessed | tf_op | source)
XLA Modules:
  0.0 48.7 jit_solution(2793793891534469760)
XLA Ops:
  1.3 45.2 %adjoint.1 = (f32[32,1024]{1,0:T(8,128)}, f32[32,1024]{1,0:T(8,128)}) custom-call(f32[128,128]{1,0:T(8,128)} %innov_hbm.1, f32[128,128]{1,0:T(8,128)} %error_hbm.1, f32[2,128,128]{2,1,0:T(8,128)} %offset_hbm.1, s32[128,128]{1,0:T(8,128)} %cell_hbm.1, s32[1,128]{1,0:T(1,128)} %owner_hbm.1, s32[1]{0:T(128)S(6)} %copy.13.count_ref, s32[32,1024]{1,0:T(8,128)} %land_hbm.1, ...), custom_call_target="tpu_custom_call" | custom-call | tf_op jit(solution)/shard_map/adjoint/pallas_call | solution.py:624
  46.4 0.0 copy-start
  46.5 1.6 %copy.14 = f32[32,1024]{1,0:T(8,128)} copy(f32[32,1024]{1,0:T(8,128)} %get-tuple-element.4) | data formatting | bytes 262144
  48.1 0.0 copy-done
  48.1 0.7 %copy.15 = f32[32,1024]{1,0:T(8,128)} copy(f32[32,1024]{1,0:T(8,128)S(1)} %copy-done) | data formatting | bytes 262144
Async XLA Ops:
  46.4 1.6 %copy-start = (f32[32,1024]{1,0:T(8,128)S(1)}, f32[32,1024]{1,0:T(8,128)}, u32[]{:S(2)}) copy-start(f32[32,1024]{1,0:T(8,128)} %get-tuple-element.5) | copy-start | bytes 393220
where the time goes:
time: 48.9 us; the launch traced here: 48.7 us
  Pallas kernels  45.2 us (92%)
  local copies, waits for them, and re-layouts  2.26 us (5%)
  between operations  1.29 us (3%)
    pallas_call x1, Pallas kernels, body(): pl.pallas_call(functools.partial(kernel, capacity), out_shape=[jax.ShapeD...  45.2 us
    unnamed x4, local copies, waits for them, and re-layouts  2.26 us

commit v1 on v0

--- a/solution.py
+++ b/solution.py
@@ -108,9 +108,6 @@
     coarse = acc_ref.shape[1]
     group_cols = cols // FINE_COL
 
-    def place(flat):
-        return (flat // (n_lon * n_obs), (flat // n_obs) % n_lon, flat % n_obs)
-
     loads = [
         pltpu.make_async_copy(source, target, in_sem.at[number])
         for number, (source, target) in enumerate(
@@ -131,13 +128,28 @@
 
     barrier = pltpu.get_barrier_semaphore()
 
-    def greet(k, carry):
-        pl.semaphore_signal(
-            barrier, inc=1, device_id=place(lax.rem(me + k, total)), device_id_type=MESH
-        )
-        return carry
-
-    lax.fori_loop(1, total, greet, 0)
+    def hop_of(ring_step):
+        odd = ring_step % 2
+        hop = odd * ((ring_step + 1) // 2) + (1 - odd) * (n_lat - ring_step // 2)
+        return hop % n_lat
+
+    def everyone(act):
+        def line_of(k, carry):
+            to_lat = lax.rem(lat + hop_of(n_lat - k), n_lat)
+            for shift in range(n_lon):
+                to_lon = lax.rem(lon + shift, n_lon)
+                for peer in range(n_obs):
+                    act((to_lat, to_lon, peer))
+            return carry
+
+        lax.fori_loop(1, n_lat, line_of, 0)
+        for shift in range(1, n_lon):
+            to_lon = lax.rem(lon + shift, n_lon)
+            for peer in range(n_obs):
+                act((lat, to_lon, peer))
+        act((lat, lon, 1 - core))
+
+    everyone(lambda device: pl.semaphore_signal(barrier, inc=1, device_id=device, device_id_type=MESH))
 
     loads[0].wait()
     count = count_ref[0]
@@ -177,16 +189,8 @@
     for load in loads[5:]:
         load.wait()
     ground_ref[0] = land_ref[...].astype(F32) * depth_ref[...]
-    pl.semaphore_wait(barrier, total - 1)
-
-    def turn_of(k):
-        ring_step, shift = k // n_lon, k % n_lon
-        odd = ring_step % 2
-        hop = odd * ((ring_step + 1) // 2) + (1 - odd) * (n_lat - ring_step // 2)
-        return hop % n_lat, shift
-
     def block_copy(k):
-        hop, shift = turn_of(k)
+        hop, shift = hop_of(k // n_lon), k % n_lon
         to_lat, to_lon = (lat + hop) % n_lat, (lon + shift) % n_lon
         return pltpu.make_async_remote_copy(
             src_ref=sent_ref.at[to_lat * n_lon + to_lon],
@@ -198,10 +202,8 @@
         )
 
     def send(k, carry):
-        block_copy(tiles - k).start()
+        block_copy(k).start()
         return carry
-
-    lax.fori_loop(1, tiles, send, 0)
 
     def halo_copy(index, source, target, device):
         return pltpu.make_async_remote_copy(
@@ -227,8 +229,6 @@
     )
     to_east = halo_copy(2, mid_ref.at[:, :, pl.ds(cols - COL_PAD, COL_PAD)], cwest_ref, (lat, east, core))
     to_west = halo_copy(3, mid_ref.at[:, :, pl.ds(0, COL_PAD)], ceast_ref, (lat, west, core))
-    to_below.start()
-    to_above.start()
 
     def post_sum(turn, parts):
         stack = jnp.concatenate(
@@ -238,18 +238,16 @@
         slot_ref[turn, pl.ds(me, 1)] = values[None]
         part_ref[turn] = values
 
-        def post(k, carry):
-            pltpu.make_async_remote_copy(
+        everyone(
+            lambda device: pltpu.make_async_remote_copy(
                 src_ref=part_ref.at[turn],
                 dst_ref=slot_ref.at[turn, me],
                 send_sem=sum_send.at[turn],
                 recv_sem=sum_recv.at[turn],
-                device_id=place(lax.rem(me + k, total)),
+                device_id=device,
                 device_id_type=MESH,
             ).start()
-            return carry
-
-        lax.fori_loop(1, total, post, 0)
+        )
 
     def take_sum(turn, number):
         block = slot_ref.at[turn, pl.ds(0, total - 1)]
@@ -286,6 +284,10 @@
         return carry
 
     lax.fori_loop(0, FINE_COL, fill, 0)
+    pl.semaphore_wait(barrier, total - 1)
+    to_below.start()
+    to_above.start()
+    lax.fori_loop(1, tiles, send, 0)
 
     def turn(k, carry):
         block_copy(k).wait_recv()
@@ -301,7 +303,7 @@
             to_east.start()
             to_west.start()
 
-        @pl.when(k == tiles // 2 - 1)
+        @pl.when(k == 3 * tiles // 4 - 1)
         def _():
             to_east.wait()
             to_west.wait()
@@ -426,17 +428,6 @@
         item.start()
     swap.start()
 
-    ocean_count, diag_sum, diag_square, face_square = take_sum(0, 4)
-    ocean_count = jnp.maximum(ocean_count, 1.0)
-    mean = diag_sum / ocean_count
-    spread_out = jnp.maximum((diag_square + face_square) / ocean_count - mean * mean, 0.0)
-    mean = 1.2 * mean
-
-    def across(value, size):
-        return jnp.concatenate([value] * (size // COL_PAD), axis=1)
-
-    diag_ref[...] = diag_ref[...] - across(mean, cols + COL_PAD)
-
     linked = jnp.where(core == 0, lat, n_lat - 1 - lat) > 0
 
     def arrived(number, target):
@@ -495,6 +486,17 @@
     q_ref[0, :, :COL_PAD] = q_ref[0, :, :COL_PAD] + entering
     q_ref[0, :, cols:] = q_ref[0, :, cols:] + beside
     q_ref[0] = q_ref[0] * ocean_ref[...]
+
+    ocean_count, diag_sum, diag_square, face_square = take_sum(0, 4)
+    ocean_count = jnp.maximum(ocean_count, 1.0)
+    mean = diag_sum / ocean_count
+    spread_out = jnp.maximum((diag_square + face_square) / ocean_count - mean * mean, 0.0)
+    mean = 1.2 * mean
+
+    def across(value, size):
+        return jnp.concatenate([value] * (size // COL_PAD), axis=1)
+
+    diag_ref[...] = diag_ref[...] - across(mean, cols + COL_PAD)
 
     spread_wide = across(spread_out, cols + COL_PAD)
     for k in range(ITERS):

time: 48.9 us -> 39.8 us (0.81)
  Pallas kernels: 45.2 us -> 36 us
    pallas_call x1, Pallas kernels: 45.2 us -> 36 us  [body(): pl.pallas_call(functools.partial(kernel, capacity), out_shape=[jax.ShapeD...]
where the time goes in v1:
time: 39.8 us; the launch traced here: 39.6 us
  Pallas kernels  36 us (90%)
  local copies, waits for them, and re-layouts  2.26 us (6%)
  between operations  1.29 us (3%)
    pallas_call x1, Pallas kernels, body(): pl.pallas_call(functools.partial(kernel, capacity), out_shape=[jax.ShapeD...  36 us
    unnamed x4, local copies, waits for them, and re-layouts  2.26 us

profile of v1, /device:TPU:0, one launch (start us, length us, event | category | flops | bytes accessed | tf_op | source)
XLA Modules:
  0.0 39.6 jit_solution(16094789607343791123)
XLA Ops:
  1.3 36.0 %adjoint.1 = (f32[32,1024]{1,0:T(8,128)}, f32[32,1024]{1,0:T(8,128)}) custom-call(f32[128,128]{1,0:T(8,128)} %innov_hbm.1, f32[128,128]{1,0:T(8,128)} %error_hbm.1, f32[2,128,128]{2,1,0:T(8,128)} %offset_hbm.1, s32[128,128]{1,0:T(8,128)} %cell_hbm.1, s32[1,128]{1,0:T(1,128)} %owner_hbm.1, s32[1]{0:T(128)S(6)} %copy.13.count_ref, s32[32,1024]{1,0:T(8,128)} %land_hbm.1, ...), custom_call_target="tpu_custom_call" | custom-call | tf_op jit(solution)/shard_map/adjoint/pallas_call | solution.py:626
  37.3 0.0 copy-start
  37.3 1.6 %copy.14 = f32[32,1024]{1,0:T(8,128)} copy(f32[32,1024]{1,0:T(8,128)} %get-tuple-element.4) | data formatting | bytes 262144
  38.9 0.0 copy-done
  38.9 0.7 %copy.15 = f32[32,1024]{1,0:T(8,128)} copy(f32[32,1024]{1,0:T(8,128)S(1)} %copy-done) | data formatting | bytes 262144
Async XLA Ops:
  37.3 1.6 %copy-start = (f32[32,1024]{1,0:T(8,128)S(1)}, f32[32,1024]{1,0:T(8,128)}, u32[]{:S(2)}) copy-start(f32[32,1024]{1,0:T(8,128)} %get-tuple-element.5) | copy-start | bytes 393220

commit v2 on v1

--- a/solution.py
+++ b/solution.py
@@ -31,7 +31,7 @@
     return -(-(FINE_ROW + 1) * (FINE_COL + 1) // 16) * 16
 
 
-def spread_block(capacity, width, cols, coarse, block):
+def operands(capacity, width, cols, coarse, block):
     fine = fine_size()
     amount = block[:, :width]
     north = block[:, width : 2 * width]
@@ -73,6 +73,15 @@
             low = jnp.where(hit, wide(rest, slot, fine), low)
         left.append(jnp.concatenate([high, low], axis=0))
         right.append(jnp.where(coarse_axis == wide(group, slot, coarse), one, zero))
+    return left, right
+
+
+def spread_blocks(capacity, width, cols, coarse, blocks):
+    left, right = [], []
+    for block in blocks:
+        more_left, more_right = operands(capacity, width, cols, coarse, block)
+        left += more_left
+        right += more_right
     return lax.dot_general(
         jnp.concatenate(left, axis=1),
         jnp.concatenate(right, axis=1),
@@ -83,12 +92,12 @@
 
 def kernel(
     capacity,
-    innov_hbm, error_hbm, offset_hbm, cell_hbm, owner_hbm, count_ref, land_hbm, inertia_hbm, depth_hbm,
+    innov_hbm, error_hbm, offset_hbm, cell_hbm, owner_hbm, count_hbm, land_hbm, inertia_hbm, depth_hbm,
     x_ref, r_ref,
-    innov_ref, error_ref, offset_ref, cell_ref, owner_ref, land_ref, depth_ref, ground_ref,
+    innov_ref, error_ref, offset_ref, cell_ref, owner_ref, count_ref, land_ref, depth_ref, ground_ref,
     sent_ref, inbox_ref, acc_ref, perm_ref,
     tile_ref, pack_ref, strip_ref, pair_ref, edge_ref, side_ref,
-    up_ref, down_ref, mid_ref, cwest_ref, ceast_ref,
+    mid_ref, cwest_ref, ceast_ref,
     ocean_ref, diag_ref, cn_ref, cs_ref, cw_ref, ce_ref, q_ref,
     part_ref, slot_ref, gram_ref,
     in_sem, send_sem, recv_sem, halo_send, halo_recv, swap_send, swap_recv, sum_send, sum_recv,
@@ -112,6 +121,7 @@
         pltpu.make_async_copy(source, target, in_sem.at[number])
         for number, (source, target) in enumerate(
             (
+                (count_hbm, count_ref),
                 (owner_hbm, owner_ref),
                 (innov_hbm, innov_ref),
                 (error_hbm, error_ref),
@@ -151,7 +161,8 @@
 
     everyone(lambda device: pl.semaphore_signal(barrier, inc=1, device_id=device, device_id_type=MESH))
 
-    loads[0].wait()
+    for load in loads[:2]:
+        load.wait()
     count = count_ref[0]
     owner_row = jnp.broadcast_to(owner_ref[...].astype(F32), (blocks, blocks))
     owner_col = owner_row.T
@@ -165,7 +176,7 @@
     slots = tiles * cap_pad
     chosen = iota((slots, blocks), 0).astype(F32) == slot_of
     chosen = jnp.where(chosen, 1.0, 0.0).astype(BF16)
-    for load in loads[1:5]:
+    for load in loads[2:6]:
         load.wait()
     error = error_ref[...]
     data = jnp.concatenate(
@@ -186,12 +197,15 @@
         jnp.concatenate([high, middle, low], axis=0),
         preferred_element_type=F32,
     ).reshape(sent_ref.shape)
-    for load in loads[5:]:
+    for load in loads[6:]:
         load.wait()
     ground_ref[0] = land_ref[...].astype(F32) * depth_ref[...]
     def block_copy(k):
         hop, shift = hop_of(k // n_lon), k % n_lon
-        to_lat, to_lon = (lat + hop) % n_lat, (lon + shift) % n_lon
+        to_lat, to_lon, bit = (lat + hop) % n_lat, 0, 1
+        while bit < n_lon:
+            to_lon = to_lon + bit * ((lon // bit + shift // bit) % 2)
+            bit = 2 * bit
         return pltpu.make_async_remote_copy(
             src_ref=sent_ref.at[to_lat * n_lon + to_lon],
             dst_ref=inbox_ref.at[k],
@@ -215,20 +229,48 @@
             device_id_type=MESH,
         )
 
-    ring = n_lat * n_obs
     line = lat * n_obs + core
-    above = lax.rem(line + ring - 1, ring)
-    below = lax.rem(line + 1, ring)
+    last_line = n_lat * n_obs - 1
+    above = jnp.maximum(line - 1, 0)
+    below = jnp.minimum(line + 1, last_line)
+    above = (above // n_obs, above % n_obs)
+    below = (below // n_obs, below % n_obs)
     west = lax.rem(lon + n_lon - 1, n_lon)
     east = lax.rem(lon + 1, n_lon)
-    to_below = halo_copy(
-        0, ground_ref.at[:, pl.ds(rows - ROW_PAD, ROW_PAD)], up_ref, (below // n_obs, lon, below % n_obs)
-    )
-    to_above = halo_copy(
-        1, ground_ref.at[:, pl.ds(0, ROW_PAD)], down_ref, (above // n_obs, lon, above % n_obs)
-    )
-    to_east = halo_copy(2, mid_ref.at[:, :, pl.ds(cols - COL_PAD, COL_PAD)], cwest_ref, (lat, east, core))
-    to_west = halo_copy(3, mid_ref.at[:, :, pl.ds(0, COL_PAD)], ceast_ref, (lat, west, core))
+    first_rows, last_rows = pl.ds(0, ROW_PAD), pl.ds(rows - ROW_PAD, ROW_PAD)
+    first_cols, last_cols = pl.ds(0, COL_PAD), pl.ds(cols - COL_PAD, COL_PAD)
+    row_before, row_after = pl.ds(0, ROW_PAD), pl.ds(keep, ROW_PAD)
+    inside = pl.ds(ROW_PAD, rows)
+
+    def across_lon(number, source_rows, target_rows, to_lat, to_core):
+        return [
+            halo_copy(
+                number,
+                ground_ref.at[:, source_rows, last_cols],
+                cwest_ref.at[:, target_rows],
+                (to_lat, east, to_core),
+            ),
+            halo_copy(
+                number + 1,
+                ground_ref.at[:, source_rows, first_cols],
+                ceast_ref.at[:, target_rows],
+                (to_lat, west, to_core),
+            ),
+        ]
+
+    level_halo = across_lon(0, pl.ds(0, rows), inside, lat, core)
+
+    def halo_above():
+        to_lat, to_core = above
+        return [
+            halo_copy(2, ground_ref.at[:, first_rows], mid_ref.at[:, row_after], (to_lat, lon, to_core))
+        ] + across_lon(3, first_rows, row_after, to_lat, to_core)
+
+    def halo_below():
+        to_lat, to_core = below
+        return [
+            halo_copy(5, ground_ref.at[:, last_rows], mid_ref.at[:, row_before], (to_lat, lon, to_core))
+        ] + across_lon(6, last_rows, row_before, to_lat, to_core)
 
     def post_sum(turn, parts):
         stack = jnp.concatenate(
@@ -259,9 +301,6 @@
             jnp.sum(gram_ref[8 * k : 8 * k + 8], axis=0, keepdims=True) for k in range(number)
         ]
 
-    def inner(value):
-        return value[ROW_PAD:keep, :cols]
-
     def fold(value):
         out = value[:8]
         for start in range(8, rows, 8):
@@ -271,8 +310,23 @@
             lanes = lanes + out[:, start : start + COL_PAD]
         return lanes
 
-    def spread(k):
-        return spread_block(capacity, width, cols, coarse, k)
+    def spread(*blocks):
+        return spread_blocks(capacity, width, cols, coarse, blocks)
+
+    pl.semaphore_wait(barrier, total - 1)
+    lax.fori_loop(1, tiles, send, 0)
+    for item in level_halo:
+        item.start()
+
+    @pl.when(line > 0)
+    def _():
+        for item in halo_above():
+            item.start()
+
+    @pl.when(line < last_line)
+    def _():
+        for item in halo_below():
+            item.start()
 
     acc_ref[...] = spread(sent_ref[lat * n_lon + lon])
 
@@ -284,55 +338,28 @@
         return carry
 
     lax.fori_loop(0, FINE_COL, fill, 0)
-    pl.semaphore_wait(barrier, total - 1)
-    to_below.start()
-    to_above.start()
-    lax.fori_loop(1, tiles, send, 0)
+
+    conduct = ground_ref[0]
+    kept = jnp.where(conduct > 0.0, 1.0, 0.0)
+    row_face = conduct * moved(conduct, 0, False)
+    col_face = conduct * moved(conduct, 1, False)
+    faces = row_face + moved(row_face, 0, True) + col_face + moved(col_face, 1, True)
+    row_face = jnp.sqrt(row_face)
+    col_face = jnp.sqrt(col_face)
+    center = ground_ref[1] + row_face + moved(row_face, 0, True) + col_face + moved(col_face, 1, True)
+    center = center * kept
+    post_sum(0, [fold(kept), fold(center), fold(center * center), fold(faces)])
+
+    block_copy(1).wait_recv()
+    acc_ref[...] = acc_ref[...] + spread(inbox_ref[1])
 
     def turn(k, carry):
-        block_copy(k).wait_recv()
-        acc_ref[...] = acc_ref[...] + spread(inbox_ref[k])
-
-        @pl.when(k == tiles // 4 - 1)
-        def _():
-            to_below.wait()
-            to_above.wait()
-            mid_ref[:, :ROW_PAD] = up_ref[...]
-            mid_ref[:, ROW_PAD:keep] = ground_ref[...]
-            mid_ref[:, keep:] = down_ref[...]
-            to_east.start()
-            to_west.start()
-
-        @pl.when(k == 3 * tiles // 4 - 1)
-        def _():
-            to_east.wait()
-            to_west.wait()
-            near = iota((tall, COL_PAD), 1) < COL_PAD // 2
-
-            def widened(index):
-                pad = jnp.where(near, ceast_ref[index], cwest_ref[index])
-                return jnp.concatenate([mid_ref[index], pad], axis=1)
-
-            conduct = widened(0)
-            cn = jnp.sqrt(conduct * moved(conduct, 0, False))
-            cs = moved(cn, 0, True)
-            cw = jnp.sqrt(conduct * moved(conduct, 1, False))
-            ce = moved(cw, 1, True)
-            ocean = jnp.where(conduct > 0.0, 1.0, 0.0)
-            diag = widened(1) + cn + cs + cw + ce
-            cn_ref[...] = cn
-            cs_ref[...] = cs
-            cw_ref[...] = cw
-            ce_ref[...] = ce
-            ocean_ref[...] = ocean
-            diag_ref[...] = diag
-            kept = inner(diag) * inner(ocean)
-            faces = cn * cn + cs * cs + cw * cw + ce * ce
-            post_sum(0, [fold(inner(ocean)), fold(kept), fold(kept * kept), fold(inner(faces))])
-
+        block_copy(2 * k).wait_recv()
+        block_copy(2 * k + 1).wait_recv()
+        acc_ref[...] = acc_ref[...] + spread(inbox_ref[2 * k], inbox_ref[2 * k + 1])
         return carry
 
-    lax.fori_loop(1, tiles, turn, 0)
+    lax.fori_loop(1, tiles // 2, turn, 0)
 
     acc_ref[:fine] = acc_ref[:fine] + acc_ref[fine:]
     step = FINE_ROW + 1
@@ -428,6 +455,48 @@
         item.start()
     swap.start()
 
+    mid_ref[:, inside] = ground_ref[...]
+
+    @pl.when(line > 0)
+    def _():
+        for item in halo_below():
+            item.wait_recv()
+
+    @pl.when(line < last_line)
+    def _():
+        for item in halo_above():
+            item.wait_recv()
+
+    @pl.when(line == 0)
+    def _():
+        for ref in (mid_ref, cwest_ref, ceast_ref):
+            ref[:, row_before] = jnp.zeros_like(ref[:, row_before])
+
+    @pl.when(line == last_line)
+    def _():
+        for ref in (mid_ref, cwest_ref, ceast_ref):
+            ref[:, row_after] = jnp.zeros_like(ref[:, row_after])
+
+    for item in level_halo:
+        item.wait_recv()
+    near = iota((tall, COL_PAD), 1) < COL_PAD // 2
+
+    def widened(index):
+        pad = jnp.where(near, ceast_ref[index], cwest_ref[index])
+        return jnp.concatenate([mid_ref[index], pad], axis=1)
+
+    conduct = widened(0)
+    cn = jnp.sqrt(conduct * moved(conduct, 0, False))
+    cs = moved(cn, 0, True)
+    cw = jnp.sqrt(conduct * moved(conduct, 1, False))
+    ce = moved(cw, 1, True)
+    cn_ref[...] = cn
+    cs_ref[...] = cs
+    cw_ref[...] = cw
+    ce_ref[...] = ce
+    ocean_ref[...] = jnp.where(conduct > 0.0, 1.0, 0.0)
+    diag_ref[...] = widened(1) + cn + cs + cw + ce
+
     linked = jnp.where(core == 0, lat, n_lat - 1 - lat) > 0
 
     def arrived(number, target):
@@ -589,8 +658,18 @@
 
     lax.fori_loop(1, tiles, finish, 0)
     swap.wait_send()
-    for item in level:
+    for item in level + level_halo:
         item.wait_send()
+
+    @pl.when(line > 0)
+    def _():
+        for item in halo_above():
+            item.wait_send()
+
+    @pl.when(line < last_line)
+    def _():
+        for item in halo_below():
+            item.wait_send()
 
     @pl.when(north)
     def _():
@@ -601,6 +680,17 @@
     def _():
         for item in southern():
             item.wait_send()
+
+
+def write(x_ref, r_ref, x_hbm, r_hbm, sem):
+    copies = [
+        pltpu.make_async_copy(x_ref, x_hbm, sem.at[0]),
+        pltpu.make_async_copy(r_ref, r_hbm, sem.at[1]),
+    ]
+    for copy in copies:
+        copy.start()
+    for copy in copies:
+        copy.wait()
 
 
 def body(
@@ -621,12 +711,11 @@
     vmem = lambda *shape: pltpu.VMEM(shape, F32)
     whole = pl.BlockSpec(memory_space=pltpu.VMEM)
     far = pl.BlockSpec(memory_space=pltpu.HBM)
-    near = pl.BlockSpec(memory_space=pltpu.SMEM)
     dma = pltpu.SemaphoreType.DMA
-    return pl.pallas_call(
+    fields = pl.pallas_call(
         functools.partial(kernel, capacity),
-        out_shape=[jax.ShapeDtypeStruct((rows, cols), F32)] * 2,
-        in_specs=[far] * 5 + [near] + [far] * 3,
+        out_shape=[pltpu.VMEM((rows, cols), F32)] * 2,
+        in_specs=[far] * 9,
         out_specs=[whole] * 2,
         scratch_shapes=[
             vmem(*innovation.shape),
@@ -634,6 +723,7 @@
             vmem(*obs_offset.shape),
             pltpu.VMEM(obs_cell.shape, jnp.int32),
             pltpu.VMEM(obs_owner.shape, jnp.int32),
+            pltpu.SMEM(block_count.shape, jnp.int32),
             pltpu.VMEM((rows, cols), jnp.int32),
             vmem(rows, cols),
             vmem(2, rows, cols),
@@ -647,8 +737,6 @@
             vmem(tall, broad),
             vmem(2, ROW_PAD, broad),
             vmem(8, 8, COL_PAD),
-            vmem(2, ROW_PAD, cols),
-            vmem(2, ROW_PAD, cols),
             vmem(2, tall, cols),
             vmem(2, tall, COL_PAD),
             vmem(2, tall, COL_PAD),
@@ -659,11 +747,11 @@
             vmem(2, 1, COL_PAD),
             vmem(2, total, 1, COL_PAD),
             vmem(COL_PAD, COL_PAD),
-            dma((8,)),
+            dma((9,)),
             dma((tiles,)),
             dma((tiles,)),
-            dma((4,)),
-            dma((4,)),
+            dma((8,)),
+            dma((8,)),
             dma((11,)),
             dma((11,)),
             dma((2,)),
@@ -675,6 +763,14 @@
         innovation, obs_error, obs_offset, obs_cell, obs_owner, block_count,
         land_mask, inertia, sea_depth,
     )
+    return pl.pallas_call(
+        write,
+        out_shape=[jax.ShapeDtypeStruct((rows, cols), F32)] * 2,
+        in_specs=[whole] * 2,
+        out_specs=[far] * 2,
+        scratch_shapes=[dma((2,))],
+        name="write",
+    )(*[pltpu.with_memory_space_constraint(field, pltpu.VMEM) for field in fields])
 
 
 def solution(mesh):

time: 39.8 us -> 36.3 us (0.912)
  local copies, waits for them, and re-layouts: 2.26 us -> 0 us
  Pallas kernels: 36 us -> 34.9 us
    unnamed x4 -> x0, local copies, waits for them, and re-layouts: 2.26 us -> none
    pallas_call x1 -> x2, Pallas kernels: 36 us -> 34.9 us  [the longest x1 34.1 us: body(): pl.pallas_call(functools.partial(kernel, capacity), out_shape=[pltpu.VMEM...]
where the time goes in v2:
time: 36.3 us; the launch traced here: 36.1 us
  Pallas kernels  34.9 us (96%)
  between operations  1.29 us (4%)
    pallas_call x1, Pallas kernels, body(): pl.pallas_call(functools.partial(kernel, capacity), out_shape=[pltpu.VMEM...  34.1 us

profile of v2, /device:TPU:0, one launch (start us, length us, event | category | flops | bytes accessed | tf_op | source)
XLA Modules:
  0.0 36.1 jit_solution(4167389844294987182)
XLA Ops:
  1.3 34.1 %adjoint.1 = (f32[32,1024]{1,0:T(8,128)S(1)}, f32[32,1024]{1,0:T(8,128)S(1)}) custom-call(f32[128,128]{1,0:T(8,128)} %innov_hbm.1, f32[128,128]{1,0:T(8,128)} %error_hbm.1, f32[2,128,128]{2,1,0:T(8,128)} %offset_hbm.1, s32[128,128]{1,0:T(8,128)} %cell_hbm.1, s32[1,128]{1,0:T(1,128)} %owner_hbm.1, s32[1]{0:T(128)S(6)} %copy.11.count_hbm, ...), custom_call_target="tpu_custom_call" | custom-call | tf_op jit(solution)/shard_map/adjoint/pallas_call | solution.py:715
  35.4 0.7 %write.1 = (f32[32,1024]{1,0:T(8,128)}, f32[32,1024]{1,0:T(8,128)}) custom-call(f32[32,1024]{1,0:T(8,128)S(1)} %get-tuple-element.4.x_ref, f32[32,1024]{1,0:T(8,128)S(1)} %get-tuple-element.5.r_ref), custom_call_target="tpu_custom_call" | custom-call | tf_op jit(solution)/shard_map/write/pallas_call | solution.py:766

commit v3 on v2

--- a/solution.py
+++ b/solution.py
@@ -206,14 +206,27 @@
         while bit < n_lon:
             to_lon = to_lon + bit * ((lon // bit + shift // bit) % 2)
             bit = 2 * bit
+        moved_over = jnp.where(k == 2, 1 - core, 0)
+        slot = k + moved_over * (tiles - 2)
         return pltpu.make_async_remote_copy(
             src_ref=sent_ref.at[to_lat * n_lon + to_lon],
+            dst_ref=inbox_ref.at[slot],
+            send_sem=send_sem.at[k],
+            recv_sem=recv_sem.at[slot],
+            device_id=(to_lat, to_lon, core + moved_over),
+            device_id_type=MESH,
+        )
+
+    def received(k):
+        pltpu.make_async_remote_copy(
+            src_ref=inbox_ref.at[k],
             dst_ref=inbox_ref.at[k],
-            send_sem=send_sem.at[k],
+            send_sem=send_sem.at[0],
             recv_sem=recv_sem.at[k],
-            device_id=(to_lat, to_lon, core),
+            device_id=(lat, lon, 1 - core),
             device_id_type=MESH,
-        )
+        ).wait_recv()
+        return inbox_ref[k]
 
     def send(k, carry):
         block_copy(k).start()
@@ -350,16 +363,30 @@
     center = center * kept
     post_sum(0, [fold(kept), fold(center), fold(center * center), fold(faces)])
 
-    block_copy(1).wait_recv()
-    acc_ref[...] = acc_ref[...] + spread(inbox_ref[1])
-
-    def turn(k, carry):
-        block_copy(2 * k).wait_recv()
-        block_copy(2 * k + 1).wait_recv()
-        acc_ref[...] = acc_ref[...] + spread(inbox_ref[2 * k], inbox_ref[2 * k + 1])
+    def gather(*slots):
+        acc_ref[...] = acc_ref[...] + spread(*[received(k) for k in slots])
+
+    @pl.when(core == 0)
+    def _():
+        gather(1)
+
+    @pl.when(core == 1)
+    def _():
+        gather(1, 2)
+
+    def two(k, carry):
+        gather(2 * k + 1, 2 * k + 2)
         return carry
 
-    lax.fori_loop(1, tiles // 2, turn, 0)
+    lax.fori_loop(1, tiles // 2 - 1, two, 0)
+
+    @pl.when(core == 0)
+    def _():
+        gather(tiles - 1)
+
+    @pl.when(core == 1)
+    def _():
+        gather(tiles - 1, tiles)
 
     acc_ref[:fine] = acc_ref[:fine] + acc_ref[fine:]
     step = FINE_ROW + 1
@@ -497,6 +524,35 @@
     ocean_ref[...] = jnp.where(conduct > 0.0, 1.0, 0.0)
     diag_ref[...] = widened(1) + cn + cs + cw + ce
 
+    ocean_count, diag_sum, diag_square, face_square = take_sum(0, 4)
+    ocean_count = jnp.maximum(ocean_count, 1.0)
+    mean = diag_sum / ocean_count
+    spread_out = jnp.maximum((diag_square + face_square) / ocean_count - mean * mean, 0.0)
+    mean = 1.2 * mean
+
+    def across(value, size):
+        return jnp.concatenate([value] * (size // COL_PAD), axis=1)
+
+    diag_ref[...] = diag_ref[...] - across(mean, cols + COL_PAD)
+
+    def finish(k, carry):
+        block_copy(k).wait_send()
+        return carry
+
+    lax.fori_loop(1, tiles, finish, 0)
+    for item in level_halo:
+        item.wait_send()
+
+    @pl.when(line > 0)
+    def _():
+        for item in halo_above():
+            item.wait_send()
+
+    @pl.when(line < last_line)
+    def _():
+        for item in halo_below():
+            item.wait_send()
+
     linked = jnp.where(core == 0, lat, n_lat - 1 - lat) > 0
 
     def arrived(number, target):
@@ -555,17 +611,6 @@
     q_ref[0, :, :COL_PAD] = q_ref[0, :, :COL_PAD] + entering
     q_ref[0, :, cols:] = q_ref[0, :, cols:] + beside
     q_ref[0] = q_ref[0] * ocean_ref[...]
-
-    ocean_count, diag_sum, diag_square, face_square = take_sum(0, 4)
-    ocean_count = jnp.maximum(ocean_count, 1.0)
-    mean = diag_sum / ocean_count
-    spread_out = jnp.maximum((diag_square + face_square) / ocean_count - mean * mean, 0.0)
-    mean = 1.2 * mean
-
-    def across(value, size):
-        return jnp.concatenate([value] * (size // COL_PAD), axis=1)
-
-    diag_ref[...] = diag_ref[...] - across(mean, cols + COL_PAD)
 
     spread_wide = across(spread_out, cols + COL_PAD)
     for k in range(ITERS):
@@ -584,6 +629,20 @@
     fields = [q_ref[k, ROW_PAD:keep, :cols] for k in range(ITERS + 1)]
     pairs = [(k, k + d) for k in range(ITERS) for d in range(2)]
     post_sum(1, [fold(fields[i] * fields[j]) for i, j in pairs])
+    swap.wait_send()
+    for item in level:
+        item.wait_send()
+
+    @pl.when(north)
+    def _():
+        for item in northern():
+            item.wait_send()
+
+    @pl.when(south)
+    def _():
+        for item in southern():
+            item.wait_send()
+
     sums = take_sum(1, len(pairs))
     gram = {}
     for (i, j), value in zip(pairs, sums):
@@ -651,35 +710,6 @@
 
     x_ref[...] = mix(gained)
     r_ref[...] = mix(resid)
-
-    def finish(k, carry):
-        block_copy(k).wait_send()
-        return carry
-
-    lax.fori_loop(1, tiles, finish, 0)
-    swap.wait_send()
-    for item in level + level_halo:
-        item.wait_send()
-
-    @pl.when(line > 0)
-    def _():
-        for item in halo_above():
-            item.wait_send()
-
-    @pl.when(line < last_line)
-    def _():
-        for item in halo_below():
-            item.wait_send()
-
-    @pl.when(north)
-    def _():
-        for item in northern():
-            item.wait_send()
-
-    @pl.when(south)
-    def _():
-        for item in southern():
-            item.wait_send()
 
 
 def write(x_ref, r_ref, x_hbm, r_hbm, sem):
@@ -728,7 +758,7 @@
             vmem(rows, cols),
             vmem(2, rows, cols),
             vmem(tiles, cap_pad, 4 * width),
-            vmem(tiles, cap_pad, 4 * width),
+            vmem(tiles + 1, cap_pad, 4 * width),
             vmem(2 * fine_size(), coarse),
             pltpu.VMEM((cols, cols), BF16),
             vmem(tile_tall, broad),
@@ -749,7 +779,7 @@
             vmem(COL_PAD, COL_PAD),
             dma((9,)),
             dma((tiles,)),
-            dma((tiles,)),
+            dma((tiles + 1,)),
             dma((8,)),
             dma((8,)),
             dma((11,)),

time: 36.3 us -> 35.7 us (0.983)
  Pallas kernels: 34.9 us -> 34.2 us
    pallas_call x1, Pallas kernels: 34.1 us -> 33.5 us  [body(): pl.pallas_call(functools.partial(kernel, capacity), out_shape=[pltpu.VMEM...]
where the time goes in v3:
time: 35.7 us; the launch traced here: 35.5 us
  Pallas kernels  34.2 us (96%)
  between operations  1.29 us (4%)
    pallas_call x1, Pallas kernels, body(): pl.pallas_call(functools.partial(kernel, capacity), out_shape=[pltpu.VMEM...  33.5 us
    pallas_call x1, Pallas kernels, body(): pl.pallas_call(write, out_shape=[jax.ShapeDtypeStruct((rows, cols), F32)]...  0.72 us

profile of v3, /device:TPU:0, one launch (start us, length us, event | category | flops | bytes accessed | tf_op | source)
XLA Modules:
  0.0 35.5 jit_solution(1879494851918016364)
XLA Ops:
  1.3 33.5 %adjoint.1 = (f32[32,1024]{1,0:T(8,128)S(1)}, f32[32,1024]{1,0:T(8,128)S(1)}) custom-call(f32[128,128]{1,0:T(8,128)} %innov_hbm.1, f32[128,128]{1,0:T(8,128)} %error_hbm.1, f32[2,128,128]{2,1,0:T(8,128)} %offset_hbm.1, s32[128,128]{1,0:T(8,128)} %cell_hbm.1, s32[1,128]{1,0:T(1,128)} %owner_hbm.1, s32[1]{0:T(128)S(6)} %copy.11.count_hbm, ...), custom_call_target="tpu_custom_call" | custom-call | tf_op jit(solution)/shard_map/adjoint/pallas_call | solution.py:745
  34.8 0.7 %write.1 = (f32[32,1024]{1,0:T(8,128)}, f32[32,1024]{1,0:T(8,128)}) custom-call(f32[32,1024]{1,0:T(8,128)S(1)} %get-tuple-element.4.x_ref, f32[32,1024]{1,0:T(8,128)S(1)} %get-tuple-element.5.r_ref), custom_call_target="tpu_custom_call" | custom-call | tf_op jit(solution)/shard_map/write/pallas_call | solution.py:796

commit v4 on v3

--- a/solution.py
+++ b/solution.py
@@ -217,7 +217,12 @@
             device_id_type=MESH,
         )
 
-    def received(k):
+    def received(turn):
+        k = jnp.where(turn == n_lon + 2, 1, turn)
+        k = jnp.where((turn > n_lon + 2) & (turn < 2 * n_lon), turn - n_lon, k)
+        k = jnp.where((turn > 2) & (turn < n_lon + 2), turn + n_lon - 2, k)
+        k = jnp.where(turn == 1, n_lon, k)
+        k = jnp.where(early, k, turn)
         pltpu.make_async_remote_copy(
             src_ref=inbox_ref.at[k],
             dst_ref=inbox_ref.at[k],
@@ -326,6 +331,12 @@
     def spread(*blocks):
         return spread_blocks(capacity, width, cols, coarse, blocks)
 
+    early = lat < (n_lat + 3) // 4
+
+    @pl.when(early)
+    def _():
+        acc_ref[...] = spread(sent_ref[lat * n_lon + lon])
+
     pl.semaphore_wait(barrier, total - 1)
     lax.fori_loop(1, tiles, send, 0)
     for item in level_halo:
@@ -341,16 +352,15 @@
         for item in halo_below():
             item.start()
 
-    acc_ref[...] = spread(sent_ref[lat * n_lon + lon])
-
-    def fill(part, carry):
-        shape = (group_cols, cols)
-        target = iota(shape, 0) * FINE_COL + part
-        start = pl.multiple_of(part * group_cols, group_cols)
-        perm_ref[pl.ds(start, group_cols)] = jnp.where(target == iota(shape, 1), 1.0, 0.0).astype(BF16)
-        return carry
-
-    lax.fori_loop(0, FINE_COL, fill, 0)
+    @pl.when(jnp.logical_not(early))
+    def _():
+        acc_ref[...] = spread(sent_ref[lat * n_lon + lon])
+
+    span = perm_ref.shape[0]
+    chunk = span // FINE_COL
+    index = iota((span, span), 0)
+    target = index % chunk * FINE_COL + index // chunk
+    perm_ref[...] = jnp.where(target == iota((span, span), 1), 1.0, 0.0).astype(BF16)
 
     conduct = ground_ref[0]
     kept = jnp.where(conduct > 0.0, 1.0, 0.0)
@@ -408,12 +418,29 @@
     lane = iota(over.shape, 1)
     planes[0] = planes[0] + jnp.where(lane > 0, over, 0.0)
     beyond = jnp.where(lane == 0, over, 0.0)
-    mixed = jnp.concatenate(planes[:FINE_COL], axis=1)
+    fit = group_cols // chunk
+    mixed = []
+    for run in range(cols // span):
+        halves = []
+        for half in range(FINE_COL // fit):
+            value = None
+            for part in range(fit):
+                shift = (part - run) % fit * chunk
+                plane = planes[half * fit + part]
+                plane = pltpu.roll(plane, shift, 1) if shift else plane
+                value = plane if part == 0 else jnp.where(lane >= part * chunk, plane, value)
+            halves.append(value)
+        mixed.append(jnp.concatenate(halves, axis=1))
+    mixed = jnp.concatenate(mixed, axis=0)
     high = mixed.astype(BF16).astype(F32)
     mixed = jnp.concatenate([high, mixed - high], axis=0).astype(BF16)
-    natural = jnp.dot(mixed, perm_ref[...], preferred_element_type=F32)
+    ordered = jnp.dot(mixed, perm_ref[...], preferred_element_type=F32)
     tile_tall = tile_rows + ROW_PAD
-    natural = natural[:tile_tall] + natural[tile_tall:]
+    runs = cols // span
+    ordered = ordered[: runs * tile_tall] + ordered[runs * tile_tall :]
+    natural = jnp.concatenate(
+        [ordered[run * tile_tall : (run + 1) * tile_tall] for run in range(runs)], axis=1
+    )
     tile_ref[:, :cols] = natural
     tile_ref[:, cols:] = beyond
     top = iota((ROW_PAD, cols + COL_PAD), 0) == 0
@@ -624,7 +651,10 @@
         )
         if k:
             value = value - spread_wide * q_ref[k - 1]
-        q_ref[k + 1] = value
+        if k < ITERS - 1:
+            q_ref[k + 1] = value
+        else:
+            q_ref[k + 1, ROW_PAD:keep, :cols] = value[ROW_PAD:keep, :cols]
 
     fields = [q_ref[k, ROW_PAD:keep, :cols] for k in range(ITERS + 1)]
     pairs = [(k, k + d) for k in range(ITERS) for d in range(2)]
@@ -760,7 +790,7 @@
             vmem(tiles, cap_pad, 4 * width),
             vmem(tiles + 1, cap_pad, 4 * width),
             vmem(2 * fine_size(), coarse),
-            pltpu.VMEM((cols, cols), BF16),
+            pltpu.VMEM((2 * COL_PAD, 2 * COL_PAD), BF16),
             vmem(tile_tall, broad),
             vmem(ROW_PAD, broad),
             vmem(COL_PAD, COL_PAD),

time: 35.7 us -> 35.5 us (level)
  no operation moved by 1% of the time
where the time goes in v4:
time: 35.5 us; the launch traced here: 35.3 us
  Pallas kernels  34 us (96%)
  between operations  1.29 us (4%)
    pallas_call x1, Pallas kernels, body(): pl.pallas_call(functools.partial(kernel, capacity), out_shape=[pltpu.VMEM...  33.3 us
    pallas_call x1, Pallas kernels, body(): pl.pallas_call(write, out_shape=[jax.ShapeDtypeStruct((rows, cols), F32)]...  0.72 us

profile of v4, /device:TPU:0, one launch (start us, length us, event | category | flops | bytes accessed | tf_op | source)
XLA Modules:
  0.0 35.3 jit_solution(2294104544083270914)
XLA Ops:
  1.3 33.3 %adjoint.1 = (f32[32,1024]{1,0:T(8,128)S(1)}, f32[32,1024]{1,0:T(8,128)S(1)}) custom-call(f32[128,128]{1,0:T(8,128)} %innov_hbm.1, f32[128,128]{1,0:T(8,128)} %error_hbm.1, f32[2,128,128]{2,1,0:T(8,128)} %offset_hbm.1, s32[128,128]{1,0:T(8,128)} %cell_hbm.1, s32[1,128]{1,0:T(1,128)} %owner_hbm.1, s32[1]{0:T(128)S(6)} %copy.11.count_hbm, ...), custom_call_target="tpu_custom_call" | custom-call | tf_op jit(solution)/shard_map/adjoint/pallas_call | solution.py:775
  34.6 0.7 %write.1 = (f32[32,1024]{1,0:T(8,128)}, f32[32,1024]{1,0:T(8,128)}) custom-call(f32[32,1024]{1,0:T(8,128)S(1)} %get-tuple-element.4.x_ref, f32[32,1024]{1,0:T(8,128)S(1)} %get-tuple-element.5.r_ref), custom_call_target="tpu_custom_call" | custom-call | tf_op jit(solution)/shard_map/write/pallas_call | solution.py:826
